TPU v7x, 32 devices: a whole 2x2x4 slice. The times are simulated.
32 devices in a mesh: seq: 16 (over z, x, core), ch: 2 (over y).
Axes of the slice: x: 2, y: 2, z: 4, core: 2. Of those that a mesh axis runs over, the one named last changes fastest.
Arguments:
- out_grad: bfloat16 [2048, 4096], P('seq', 'ch'), may hold values from -6 to 6
- out_weight: bfloat16 [4096, 4096], P(('seq', 'ch')), may hold values from -0.09375 to 0.09375
- outer_gate: bfloat16 [2048, 4096], P('seq', 'ch'), may hold values from -6 to 6
- long_out: bfloat16 [2048, 4096], P('seq', 'ch'), may hold values from -6 to 6
- inner_gate: bfloat16 [2048, 4096], P('seq', 'ch'), may hold values from -6 to 6
- conv_input: bfloat16 [2048, 4096], P('seq', 'ch'), may hold values from -6 to 6
- short_out: bfloat16 [2048, 4096], P('seq', 'ch'), may hold values from -6 to 6
- medium_out: bfloat16 [2048, 4096], P('seq', 'ch'), may hold values from -6 to 6
- long_filter: bfloat16 [2048, 4096], P('seq', 'ch'), may hold values from -6 to 6
- taps_short: bfloat16 [7, 4096], P(None, 'ch'), may hold values from -2 to 2
- taps_medium: bfloat16 [128, 4096], P(None, 'ch'), may hold values from -0.5 to 0.5
Outputs:
- grad_outer: bfloat16 [2048, 4096], P('seq', 'ch')
- grad_inner: bfloat16 [2048, 4096], P('seq', 'ch')
- grad_input: bfloat16 [2048, 4096], P('seq', 'ch')
- grad_filter: float32 [2048, 4096], P('seq', 'ch')
- grad_short: float32 [7, 4096], P(None, 'ch')
- grad_medium: float32 [128, 4096], P(None, 'ch')
All inputs are finite; a program needn't handle non-finite values.
Results may differ from a plain program's by a relative error of at most 0.0065.
Values may be sent and summed in bfloat16 or wider, within the bound.
No kernel may reach another device: no remote copies, remote signals or barrier semaphores. Data moves between devices by JAX's collectives and lax.ppermute only.
A program may use at most 128 MiB of HBM per device.

v0:
```python
import math

import jax
import jax.numpy as jnp
from jax import lax
from jax.sharding import PartitionSpec as P

SHORT = 7
MEDIUM = 128


ACCURATE = lax.Precision.HIGH


def from_behind(value, axis, steps):
    count = lax.axis_size(axis)
    leading, last = (max(0, -steps), min(count, count - steps))
    return lax.ppermute(value, axis, [(source, source + steps) for source in range(leading, last)])


def rotation(numer, denom):
    angles = 2.0 * math.pi / denom * numer.astype(jnp.float32)
    return (jnp.cos(angles), jnp.sin(angles))


def dft_table(length, orient):
    indices = lax.iota(jnp.int32, length)
    cosine, sine_part = rotation(indices[:, None] * indices[None, :] % length, length)
    return (cosine, orient * sine_part)


def apply_table(table, real_part, imag_part, pattern):

    def multiply(left, right):
        return jnp.einsum(pattern, left, right, precision=ACCURATE)

    if imag_part is None:
        return (multiply(table[0], real_part), multiply(table[1], real_part))
    return (
        multiply(table[0], real_part) - multiply(table[1], imag_part),
        multiply(table[0], imag_part) + multiply(table[1], real_part),
    )


def real_table(table, real_part, imag_part, pattern):
    return jnp.einsum(pattern, table[0], real_part, precision=ACCURATE) - jnp.einsum(
        pattern, table[1], imag_part, precision=ACCURATE
    )


def twist(real_part, imag_part, cosine, sine_part):
    return (real_part * cosine - imag_part * sine_part, real_part * sine_part + imag_part * cosine)


def outer_forward(signal, time_pos, row_pos, freq_pos, total):
    table = dft_table(signal.shape[0], -1.0)
    cosine, sine_part = rotation(time_pos, 2 * total)
    shift_real, shift_imag = rotation(row_pos * freq_pos % total, total)
    outputs = []
    for parity in range(2):
        if parity == 0:
            real_part, imag_part = apply_table(table, signal, None, "ca,am->cm")
        else:
            real_part, imag_part = apply_table(
                table, signal * cosine, -signal * sine_part, "ca,am->cm"
            )
        outputs += list(twist(real_part, imag_part, shift_real, -shift_imag))
    return outputs


def inner_forward(parts):
    table = dft_table(parts[0].shape[0], -1.0)
    outputs = []
    for place in range(0, len(parts), 2):
        outputs += list(apply_table(table, parts[place], parts[place + 1], "br,rn->bn"))
    return outputs


def inner_inverse(parts, narrow, total):
    table = dft_table(parts[0].shape[0], 1.0)
    row_pos = lax.iota(jnp.int32, parts[0].shape[0])[:, None]
    freq_pos = lax.iota(jnp.int32, parts[0].shape[1])[None, :] // narrow
    shift_real, shift_imag = rotation(row_pos * freq_pos % total, total)
    outputs = []
    for place in range(0, len(parts), 2):
        real_part, imag_part = apply_table(table, parts[place], parts[place + 1], "rb,bn->rn")
        outputs += list(twist(real_part, imag_part, shift_real, shift_imag))
    return outputs


def outer_inverse(parts, time_pos, total):
    table = dft_table(parts[0].shape[0], 1.0)
    cosine, sine_part = rotation(time_pos, 2 * total)
    outputs = []
    for place in range(0, len(parts), 4):
        high_real, high_imag = apply_table(table, parts[place + 2], parts[place + 3], "ac,cm->am")
        high_real, high_imag = twist(high_real, high_imag, cosine, sine_part)
        outputs.append(real_table(table, parts[place], parts[place + 1], "ac,cm->am") + high_real)
    return outputs


def conj_times(left_real, left_imag, right_real, right_imag):
    return (
        left_real * right_real + left_imag * right_imag,
        left_real * right_imag - left_imag * right_real,
    )


def spectral_terms(spectra):
    first, second = ([], [])
    for parity in range(2):
        grad_real, grad_imag = (spectra[4 + 2 * parity], spectra[5 + 2 * parity])
        point_real, point_imag = conj_times(
            spectra[8 + 2 * parity], spectra[9 + 2 * parity], grad_real, grad_imag
        )
        filt_real, filt_imag = conj_times(
            spectra[2 * parity], spectra[2 * parity + 1], grad_real, grad_imag
        )
        first += [point_real, point_imag]
        second += [filt_real, filt_imag]
    return first + second


def depthwise(signal, kernel):
    channels = signal.shape[1]
    result = lax.conv_general_dilated(
        signal.astype(jnp.float32)[None],
        kernel.astype(jnp.float32)[:, None, :],
        (1,),
        "VALID",
        dimension_numbers=("NWC", "WIO", "NWC"),
        feature_group_count=channels,
        precision=lax.Precision.HIGHEST,
    )
    return result[0]


def adjoint_taps(extended, taps):
    return depthwise(extended, taps)


def tap_products(grads, extended):
    return depthwise(extended, grads)[::-1]


def per_device(
    out_grad,
    out_weight,
    outer_gate,
    long_out,
    inner_gate,
    conv_input,
    short_out,
    medium_out,
    long_filter,
    taps_short,
    taps_medium,
):
    height = out_grad.shape[0]
    channels = outer_gate.shape[1]
    devices = lax.axis_size("seq")
    total = height * devices
    earlier_short, earlier_input = from_behind(
        (short_out[height - (MEDIUM - 1) :], conv_input[height - (SHORT - 1) :]), "seq", 1
    )
    features = lax.all_gather(out_grad, "ch", axis=1, tiled=True)
    aligned = lax.all_to_all(out_weight, "ch", split_axis=1, concat_axis=0, tiled=True)
    hidden = jnp.dot(
        features,
        lax.all_gather(aligned, "seq", axis=0, tiled=True),
        preferred_element_type=jnp.float32,
    )
    grad_outer = (hidden * long_out.astype(jnp.float32)).astype(jnp.bfloat16)
    long_grad = (hidden * outer_gate.astype(jnp.float32)).astype(jnp.bfloat16)
    product = (inner_gate.astype(jnp.float32) * medium_out.astype(jnp.float32)).astype(jnp.bfloat16)
    narrow = channels // devices
    lane_span = height * narrow

    def to_blocks(signal):
        return (
            signal.reshape(height, devices, narrow).transpose(1, 0, 2).reshape(devices, lane_span)
        )

    def to_inner(signal):
        return (
            signal.reshape(devices, height, narrow)
            .transpose(1, 0, 2)
            .reshape(height, devices * narrow)
        )

    arrived = (
        lax.all_to_all(to_blocks(product), "seq", split_axis=0, concat_axis=0, tiled=True),
        lax.all_to_all(to_blocks(long_grad), "seq", split_axis=0, concat_axis=0, tiled=True),
        lax.all_to_all(to_blocks(long_filter), "seq", split_axis=0, concat_axis=0, tiled=True),
    )
    row_pos = lax.iota(jnp.int32, lane_span)[None, :] // narrow
    source = lax.iota(jnp.int32, devices)[:, None]
    time_pos = source * height + row_pos
    spread = []
    for signal in arrived:
        spread += outer_forward(signal.astype(jnp.float32), time_pos, row_pos, source, total)
    spectra = inner_forward([to_inner(piece) for piece in spread])
    terms = inner_inverse(spectral_terms(spectra), narrow, total)
    results = outer_inverse([to_blocks(piece) for piece in terms], time_pos, total)
    result = lax.all_to_all(jnp.stack(results), "seq", split_axis=1, concat_axis=1, tiled=True)
    result = (
        result.reshape(2, devices, height, narrow)
        .transpose(0, 2, 1, 3)
        .reshape(2, height, channels)
    )
    scale = total ** (-0.5) / (2.0 * total)
    point_grad = result[0] * scale
    grad_filter = result[1] * scale
    medium_grad = (point_grad * inner_gate.astype(jnp.float32)).astype(jnp.bfloat16)
    grad_inner = (point_grad * medium_out.astype(jnp.float32)).astype(jnp.bfloat16)
    later_medium = from_behind(medium_grad[: MEDIUM - 1], "seq", -1)
    short_grad = adjoint_taps(jnp.concatenate([medium_grad, later_medium]), taps_medium).astype(
        jnp.bfloat16
    )
    later_short = from_behind(short_grad[: SHORT - 1], "seq", -1)
    grad_input = adjoint_taps(jnp.concatenate([short_grad, later_short]), taps_short).astype(
        jnp.bfloat16
    )
    partial_medium = tap_products(medium_grad, jnp.concatenate([earlier_short, short_out]))
    partial_short = tap_products(short_grad, jnp.concatenate([earlier_input, conv_input]))
    sum_medium, sum_short = lax.psum((partial_medium, partial_short), "seq")
    factor = total ** (-0.5)
    return (
        grad_outer,
        grad_inner,
        grad_input,
        grad_filter,
        sum_short * factor,
        sum_medium * factor,
    )


def solution(mesh):
    return jax.shard_map(
        per_device,
        mesh=mesh,
        in_specs=(
            P("seq", "ch"),
            P(("seq", "ch"), None),
            P("seq", "ch"),
            P("seq", "ch"),
            P("seq", "ch"),
            P("seq", "ch"),
            P("seq", "ch"),
            P("seq", "ch"),
            P("seq", "ch"),
            P(None, "ch"),
            P(None, "ch"),
        ),
        out_specs=(
            P("seq", "ch"),
            P("seq", "ch"),
            P("seq", "ch"),
            P("seq", "ch"),
            P(None, "ch"),
            P(None, "ch"),
        ),
        check_vma=False,
    )
```

profile of v0, /device:TPU:0, one launch (start us, length us, event | category | flops | bytes accessed | tf_op | source)
XLA Modules:
  0.0 585.1 jit_solution(104122376312642344)
XLA Ops:
  9.6 24.2 %all_to_all.63 = bf16[128,2,2048]{0,2,1:T(8,128)(2,1)S(1)} all-to-all(bf16[128,2,2048]{0,2,1:T(8,128)(2,1)S(1)} %bitcast.387), channel_id=1, replica_groups=mesh['seq'=16,'ch'=2] {'ch'}, dimensions={1} | all-to-all | bytes 2097152 | tf_op jit(solution)/shard_map/all_to_all | solution.py:167
  41.0 6.4 %all-to-all-start.1 = ((bf16[16,2,8192]{2,1,0:T(2,128)(2,1)}), bf16[16,2,8192]{2,1,0:T(2,128)(2,1)S(1)}, u32[]{:S(2)}, u32[]{:S(2)}) async-start(bf16[16,2,8192]{2,1,0:T(2,128)(2,1)} %reshape.319), calls=%async_computation.1 | async-start | bytes 1048576 | tf_op jit(solution)/shard_map/all_to_all | solution.py:194
  53.8 13.7 %all-to-all-done.1 = bf16[16,2,8192]{2,1,0:T(2,128)(2,1)S(1)} async-done(((bf16[16,2,8192]{2,1,0:T(2,128)(2,1)}), bf16[16,2,8192]{2,1,0:T(2,128)(2,1)S(1)}, u32[]{:S(2)}, u32[]{:S(2)}) %all-to-all-start.1) | async-done | bytes 524320 | tf_op jit(solution)/shard_map/all_to_all | solution.py:194
  67.6 11.8 %all-to-all-start.3 = ((bf16[16,2,8192]{2,1,0:T(2,128)(2,1)}), bf16[16,2,8192]{2,1,0:T(2,128)(2,1)S(1)}, u32[]{:S(2)}, u32[]{:S(2)}) async-start(bf16[16,2,8192]{2,1,0:T(2,128)(2,1)} %reshape.315), calls=%async_computation.3 | async-start | bytes 1048576 | tf_op jit(solution)/shard_map/all_to_all | solution.py:192
  80.5 21.9 %all-to-all-done.3 = bf16[16,2,8192]{2,1,0:T(2,128)(2,1)S(1)} async-done(((bf16[16,2,8192]{2,1,0:T(2,128)(2,1)}), bf16[16,2,8192]{2,1,0:T(2,128)(2,1)S(1)}, u32[]{:S(2)}, u32[]{:S(2)}) %all-to-all-start.3) | async-done | bytes 524320 | tf_op jit(solution)/shard_map/all_to_all | solution.py:192
  105.5 4.1 fusion.71
  109.6 5.1 fusion.56
  114.8 5.2 fusion.65
  119.9 5.5 fusion.58
  125.4 5.1 convolution_add_fusion.4
  130.5 56.4 %all-gather.5.cloned.1.call-done = bf16[4096,2048]{1,0:T(8,128)(2,1)} async-done(((bf16[256,2048]{1,0:T(8,128)(2,1)}), bf16[4096,2048]{1,0:T(8,128)(2,1)}) %all-gather.5.cloned.1.call-update) | async-done | bytes 16777232 | tf_op jit(solution)/shard_map/all_gather | solution.py:170
  186.9 9.4 %fusion.88 = (bf16[16,16,8,128]{3,2,1,0:T(8,128)(2,1)S(1)}, bf16[128,2048]{1,0:T(8,128)(2,1)}) fusion(bf16[128,2048]{1,0:T(8,128)(2,1)S(1)} %copy-done.50, bf16[128,2048]{1,0:T(8,128)(2,1)} %param.14, bf16[128,4096]{1,0:T(8,128)(2,1)} %all-gather.3.cloned.1.call-done, bf16[4096,2048]{1,0:T(8,128)(2,1)} %all-gather.5.cloned.1.call-done), kind=kOutput, calls=%fused_computation.181 | convolution fusion | flops 2149056512 | bytes 19922944 | tf_op jit(solution)/shard_map/dot_general | solution.py:168
  198.1 4.9 reduce.1
  204.2 4.2 all-to-all-start.2
  210.0 6.6 %convolution_subtract_fusion.5 = f32[16,16384]{1,0:T(8,128)} fusion(f32[16,16384]{1,0:T(8,128)} %fusion.56, bf16[16,1,16384]{2,0,1:T(8,128)(2,1)S(1)} %copy.177, s32[16]{0:T(128)S(1)} %iota_multiply_fusion, s32[16384]{0:T(1024)S(1)} %add_select_fusion.2), kind=kOutput, calls=%fused_computation.20 | convolution fusion | flops 27004672 | bytes 2687040 | tf_op jit(solution)/shard_map/ca,am->cm/dot_general | solution.py:35
  216.6 5.1 convolution_add_fusion.1
  221.7 5.2 convolution_subtract_fusion.1
  239.0 4.3 convolution_add_fusion.3
  243.3 4.1 convolution_subtract_fusion.4
  247.5 8.8 %subtract_bitcast_fusion.6 = (f32[2,8,128,128]{3,1,2,0:T(8,128)}, f32[2,8,128,128]{3,1,2,0:T(8,128)}, f32[2,8,128,128]{3,1,2,0:T(8,128)}, f32[2,8,128,128]{3,1,2...) fusion(f32[16,16384]{1,0:T(8,128)S(1)} %copy-done.16, ...), kind=kOutput, calls=%fused_computation.139 | convolution fusion | flops 38538752 | bytes 24707072 | tf_op jit(solution)/shard_map/ca,am->cm/dot_general | solution.py:35
  347.9 5.7 add_bitcast_fusion.4
  357.5 4.4 fusion.4
  365.7 4.8 fusion.9
  372.6 4.5 fusion.3
  377.1 4.7 fusion.8
  384.9 6.0 %all-to-all-start.4 = ((f32[2,16,16384]{2,0,1:T(2,128)}), f32[2,16,16384]{2,0,1:T(2,128)S(1)}, u32[]{:S(2)}, u32[]{:S(2)}) async-start(f32[2,16,16384]{2,0,1:T(2,128)} %copy.165), calls=%async_computation.4 | async-start | bytes 4194304 | tf_op jit(solution)/shard_map/all_to_all | solution.py:205
  401.7 30.2 %all-to-all-done.4 = f32[2,16,16384]{2,0,1:T(2,128)S(1)} async-done(((f32[2,16,16384]{2,0,1:T(2,128)}), f32[2,16,16384]{2,0,1:T(2,128)S(1)}, u32[]{:S(2)}, u32[]{:S(2)}) %all-to-all-start.4) | async-done | bytes 2097184 | tf_op jit(solution)/shard_map/all_to_all | solution.py:205
  441.3 14.9 %fusion.11 = f32[1,128,2048]{2,0,1:T(1,128)S(1)} fusion(bf16[1,255,2048]{2,1,0:T(8,128)(2,1)S(1)} %copy-done.48, bf16[128,1,2048]{2,0,1:T(8,128)(2,1)S(1)} %bitcast.394), kind=kOutput, calls=%fused_computation.47 | convolution fusion | flops 67108864 | bytes 2617344 | tf_op jit(solution)/shard_map/conv_general_dilated | solution.py:126
  457.9 5.2 rev.7
  463.2 14.8 %convolution_convert_fusion = bf16[1,128,2048]{2,0,1:T(2,128)(2,1)S(1)} fusion(bf16[1,255,2048]{2,1,0:T(8,128)(2,1)S(1)} %maximum_bitcast_fusion, bf16[128,1,2048]{2,0,1:T(8,128)(2,1)S(1)} %bitcast.335), kind=kOutput, calls=%fused_computation.43 | convolution fusion | flops 67371008 | bytes 2093056 | tf_op jit(solution)/shard_map/conv_general_dilated | solution.py:126
  482.6 68.9 %psum.14 = f32[7,2048]{1,0:T(8,128)S(1)} all-reduce(f32[7,2048]{1,0:T(8,128)S(1)} %rev.6), channel_id=1, replica_groups=mesh['seq'=16,'ch'=2] {'seq'}, use_global_device_ids=true, to_apply=%region_0.1 | all-reduce | flops 14336 | bytes 114688 | tf_op jit(solution)/shard_map/psum | solution.py:226
  552.2 21.0 %all-reduce.2.cloned.1.call-done = f32[128,2048]{1,0:T(8,128)} async-done(((f32[128,2048]{1,0:T(8,128)}), f32[128,2048]{1,0:T(8,128)}) %all-reduce.2.cloned.1.call-update) | async-done | bytes 1048592 | tf_op jit(solution)/shard_map/psum | solution.py:226
  (259 shorter events, 172.9 us)
Async XLA Ops:
  7.2 456.0 %copy-start = (bf16[128,2048]{1,0:T(8,128)(2,1)S(1)}, bf16[128,2048]{1,0:T(8,128)(2,1)}, u32[]{:S(2)}) copy-start(bf16[128,2048]{1,0:T(8,128)(2,1)} %param.21) | copy-start | bytes 1572868
  7.2 123.3 %all-gather.3.cloned.1.call-start = ((), (), s32[]{:S(2)}) async-start(), calls=%async_computation.5 | async-start | bytes 1572864 | tf_op jit(solution)/shard_map/all_gather | solution.py:166
  7.9 179.0 %all-gather.5.cloned.1.call-start = ((), (), s32[]{:S(2)}) async-start(), calls=%async_computation.6 | async-start | bytes 17825792 | tf_op jit(solution)/shard_map/all_gather | solution.py:170
  35.5 11.9 %copy-start.44 = (bf16[128,2048]{1,0:T(8,128)(2,1)S(1)}, bf16[128,2048]{1,0:T(8,128)(2,1)}, u32[]{:S(2)}) copy-start(bf16[128,2048]{1,0:T(8,128)(2,1)} %param.15) | copy-start | bytes 1572868
  41.0 26.6 %all-to-all-start.1 = ((bf16[16,2,8192]{2,1,0:T(2,128)(2,1)}), bf16[16,2,8192]{2,1,0:T(2,128)(2,1)S(1)}, u32[]{:S(2)}, u32[]{:S(2)}) async-start(bf16[16,2,8192]{2,1,0:T(2,128)(2,1)} %reshape.319), calls=%async_computation.1 | async-start | bytes 1048576 | tf_op jit(solution)/shard_map/all_to_all | solution.py:194
  67.6 34.9 %all-to-all-start.3 = ((bf16[16,2,8192]{2,1,0:T(2,128)(2,1)}), bf16[16,2,8192]{2,1,0:T(2,128)(2,1)S(1)}, u32[]{:S(2)}, u32[]{:S(2)}) async-start(bf16[16,2,8192]{2,1,0:T(2,128)(2,1)} %reshape.315), calls=%async_computation.3 | async-start | bytes 1048576 | tf_op jit(solution)/shard_map/all_to_all | solution.py:192
  119.9 67.0 %copy-start.50 = (bf16[128,2048]{1,0:T(8,128)(2,1)S(1)}, bf16[128,2048]{1,0:T(8,128)(2,1)}, u32[]{:S(2)}) copy-start(bf16[128,2048]{1,0:T(8,128)(2,1)} %param.13) | copy-start | bytes 1572868
  204.2 22.7 %all-to-all-start.2 = ((bf16[16,2,8192]{2,1,0:T(2,128)(2,1)}), bf16[16,2,8192]{2,1,0:T(2,128)(2,1)}, u32[]{:S(2)}, u32[]{:S(2)}) async-start(bf16[16,2,8192]{2,1,0:T(2,128)(2,1)} %reshape.317), calls=%async_computation.2 | async-start | bytes 1048576 | tf_op jit(solution)/shard_map/all_to_all | solution.py:193
  208.4 8.2 %copy-start.35 = (f32[16,16384]{1,0:T(8,128)S(1)}, f32[16,16384]{1,0:T(8,128)}, u32[]{:S(2)}) copy-start(f32[16,16384]{1,0:T(8,128)} %fusion.65) | copy-start | bytes 3145732
  210.0 11.7 %copy-start.34 = (f32[16,16384]{1,0:T(8,128)S(1)}, f32[16,16384]{1,0:T(8,128)}, u32[]{:S(2)}) copy-start(f32[16,16384]{1,0:T(8,128)} %fusion.58) | copy-start | bytes 3145732
  234.9 12.5 %copy-start.22 = (f32[16,16384]{1,0:T(8,128)S(1)}, f32[16,16384]{1,0:T(8,128)}, u32[]{:S(2)}) copy-start(f32[16,16384]{1,0:T(8,128)} %convolution_subtract_fusion.1) | copy-start | bytes 3145732
  239.0 8.4 %copy-start.15 = (f32[16,16384]{1,0:T(8,128)S(1)}, f32[16,16384]{1,0:T(8,128)}, u32[]{:S(2)}) copy-start(f32[16,16384]{1,0:T(8,128)} %fusion.96) | copy-start | bytes 3145732
  239.0 8.4 %copy-start.16 = (f32[16,16384]{1,0:T(8,128)S(1)}, f32[16,16384]{1,0:T(8,128)}, u32[]{:S(2)}) copy-start(f32[16,16384]{1,0:T(8,128)} %convolution_add_fusion.4) | copy-start | bytes 3145732
  239.0 8.4 %copy-start.19 = (f32[16,16384]{1,0:T(8,128)S(1)}, f32[16,16384]{1,0:T(8,128)}, u32[]{:S(2)}) copy-start(f32[16,16384]{1,0:T(8,128)} %fusion.110) | copy-start | bytes 3145732
  239.0 8.4 %copy-start.20 = (f32[16,16384]{1,0:T(8,128)S(1)}, f32[16,16384]{1,0:T(8,128)}, u32[]{:S(2)}) copy-start(f32[16,16384]{1,0:T(8,128)} %convolution_subtract_fusion.5) | copy-start | bytes 3145732
  239.0 8.4 %copy-start.21 = (f32[16,16384]{1,0:T(8,128)S(1)}, f32[16,16384]{1,0:T(8,128)}, u32[]{:S(2)}) copy-start(f32[16,16384]{1,0:T(8,128)} %convolution_add_fusion.1) | copy-start | bytes 3145732
  257.5 3.5 copy-start.25
  270.1 3.0 copy-start.5
  281.3 3.5 copy-start.17
  301.1 3.4 copy-start.13
  313.8 3.0 copy-start.3
  322.0 2.1 copy-start.10
  325.3 3.5 copy-start.9
  384.9 6.1 %copy-start.47 = (bf16[128,2048]{1,0:T(8,128)(2,1)S(1)}, bf16[128,2048]{1,0:T(8,128)(2,1)}, u32[]{:S(2)}) copy-start(bf16[128,2048]{1,0:T(8,128)(2,1)} %param.17) | copy-start | bytes 1572868
  384.9 47.0 %all-to-all-start.4 = ((f32[2,16,16384]{2,0,1:T(2,128)}), f32[2,16,16384]{2,0,1:T(2,128)S(1)}, u32[]{:S(2)}, u32[]{:S(2)}) async-start(f32[2,16,16384]{2,0,1:T(2,128)} %copy.165), calls=%async_computation.4 | async-start | bytes 4194304 | tf_op jit(solution)/shard_map/all_to_all | solution.py:205
  390.9 182.2 %all-reduce.2.cloned.1.call-start = ((), (), s32[]{:S(2)}) async-start(), calls=%async_computation.7 | async-start | bytes 2097152 | tf_op jit(solution)/shard_map/psum | solution.py:226
  391.1 9.5 %collective-permute-start.3 = (bf16[127,2048]{1,0:T(8,128)(2,1)S(1)}, bf16[127,2048]{1,0:T(8,128)(2,1)S(1)}, u32[]{:S(2)}, u32[]{:S(2)}) collective-permute-start(bf16[127,2048]{1,0:T(8,128)(2,1)S(1)} %slice.29), channel_id=1, source_target_pairs={{0,2},{2,4},{4,6},{6,8},{8,10},{10,12},{12,14},{14,16},{16,18},{18... | collective-permute-start | bytes 1560584 | tf_op jit(solution)/shard_map/ppermute | solution.py:18
  394.3 4.4 collective-permute-start.2
  437.7 3.6 copy-start.48
  440.0 23.0 %collective-permute-start = (bf16[127,2048]{1,0:T(8,128)(2,1)S(1)}, bf16[127,2048]{1,0:T(8,128)(2,1)S(1)}, u32[]{:S(2)}, u32[]{:S(2)}) collective-permute-start(bf16[127,2048]{1,0:T(8,128)(2,1)S(1)} %bitcast.393), channel_id=1, source_target_pairs={{2,0},{4,2},{6,4},{8,6},{10,8},{12,10},{14,12},{16,14},{18,16},{20... | collective-permute-start | bytes 1560584 | tf_op jit(solution)/shard_map/ppermute | solution.py:18
  463.2 16.6 %copy-start.49 = (bf16[1,134,2048]{2,1,0:T(8,128)(2,1)S(1)}, bf16[1,134,2048]{2,1,0:T(8,128)(2,1)}, u32[]{:S(2)}) copy-start(bf16[1,134,2048]{2,1,0:T(8,128)(2,1)} %maximum_bitcast_fusion.3) | copy-start | bytes 1646596
  478.4 97.0 %collective-permute-start.1 = (bf16[6,2048]{1,0:T(8,128)(2,1)S(1)}, bf16[6,2048]{1,0:T(8,128)(2,1)S(1)}, u32[]{:S(2)}, u32[]{:S(2)}) collective-permute-start(bf16[6,2048]{1,0:T(8,128)(2,1)S(1)} %bitcast.397), channel_id=1, source_target_pairs={{2,0},{4,2},{6,4},{8,6},{10,8},{12,10},{14,12},{16,14},{18,16},{20... | collective-permute-start | bytes 73736 | tf_op jit(solution)/shard_map/ppermute | solution.py:18
  (33 other events, 52.7 us)
Sparse Core Ops, SparseCore 0:
  9.5 29.1 all-gather.2
  41.5 145.4 all-gather.4
  463.2 109.9 all-reduce.1
where the time goes:
time: 593 us; the launch traced here: 585 us
  matrix products  200 us (34%)
  waiting for transfers between devices  145 us (24%)
  blocking collectives  93 us (16%)
  local copies, waits for them, and re-layouts  73.2 us (12%)
  starting transfers between devices  37 us (6%)
  other arithmetic  21.5 us (4%)
  between operations  15.2 us (3%)
    dot_general x66, matrix products, multiply(): return jnp.einsum(pattern, left, right, precision=ACCURATE)  154 us
    psum x1, blocking collectives, per_device(): sum_medium, sum_short = lax.psum((partial_medium, partial_short), 'seq')  68.9 us
    all_gather x1, waiting for transfers between devices, per_device(): lax.all_gather(aligned, 'seq', axis=0, tiled=True)  56.4 us
    conv_general_dilated x4, matrix products, depthwise(): lax.conv_general_dilated(signal.astype(jnp.float32)[None], kernel.astype(...  32.9 us
    unnamed x135, local copies, waits for them, and re-layouts  31.9 us
    all_to_all x1, waiting for transfers between devices, per_device(): lax.all_to_all(jnp.stack(results), 'seq', split_axis=1, concat_axis=1, ti...  30.2 us
    all_to_all x1, blocking collectives, per_device(): lax.all_to_all(out_weight, 'ch', split_axis=1, concat_axis=0, tiled=True)  24.2 us
    all_to_all x1, waiting for transfers between devices, per_device(): lax.all_to_all(to_blocks(product), 'seq', split_axis=0, concat_axis=0, ti...  21.9 us
  transfers between devices with their start and end apart: 11, of which 6 were waited for; matrix products, arithmetic and copies ran while one was open for 19% of the time, Pallas kernels for 0%

commit v1 on v0

v1 whole, which is shorter than its diff:
```python
import functools
import math

import jax
import jax.numpy as jnp
from jax import lax
from jax.experimental import pallas as pl
from jax.experimental.pallas import tpu as pltpu
from jax.sharding import Mesh, PartitionSpec as P


BLOCK = 256
UNROLL = 8
LANES = 128
SUB = 8
BF16 = jnp.bfloat16
F32 = jnp.float32
VMEM_LIMIT = 60 * 1024 * 1024


def table(block):
    row = lax.iota(jnp.int32, 2 * block)[:, None]
    slot = row % block
    freq = jnp.where(slot < block // 2, 2 * slot, 2 * (slot - block // 2) + 1)
    time = lax.iota(jnp.int32, block)[None, :]
    angle = (((2 * freq + 1) * time) % (4 * block)).astype(F32) * (math.pi / (2 * block))
    full = jnp.where(row < block, jnp.cos(angle), -jnp.sin(angle))
    high = lax.reduce_precision(full, 8, 7)
    low = full - high
    return high.astype(BF16), low.astype(BF16)


def dot(left, right):
    return jnp.dot(left, right, preferred_element_type=F32)


def forward(ftab_ref, value):
    both = dot(ftab_ref[...], value)
    half = both.shape[0] // 2
    return both[:half] + both[half:]


def inverse(itab_ref, spectrum, count):
    high = spectrum.astype(BF16)
    low = (spectrum - high.astype(F32)).astype(BF16)
    both = dot(itab_ref[...], high)
    return both[:count] + both[count:] + dot(itab_ref[:count], low)


def each(count, body):
    if count <= UNROLL:
        for index in range(count):
            body(index)
    else:

        def step(index, carry):
            body(index)
            return carry

        lax.fori_loop(0, count, step, 0)


def join(spec_ref):
    blocks, double, _ = spec_ref.shape
    block = double // 2

    def chunk(r, carry):
        rows = pl.ds(pl.multiple_of(r * SUB, SUB), SUB)
        irows = pl.ds(pl.multiple_of(block + r * SUB, SUB), SUB)
        sign = jnp.where(r < block // (2 * SUB), 1.0, -1.0).astype(F32)

        def step(s):
            real = spec_ref[s + 1, rows, :]
            imag = spec_ref[s + 1, irows, :]
            spec_ref[s, rows, :] = spec_ref[s, rows, :] + sign * imag
            spec_ref[s, irows, :] = spec_ref[s, irows, :] - sign * real

        each(blocks - 1, step)
        return carry

    lax.fori_loop(0, block // SUB, chunk, 0)


def conj_times(left, right):
    return left[0] * right[0] + left[1] * right[1], left[0] * right[1] - left[1] * right[0]


def correlate(spec_ref, joined_ref, hold_ref):
    blocks, double, lanes = spec_ref.shape
    block = double // 2

    def chunk(r, carry):
        rows = pl.ds(pl.multiple_of(r * SUB, SUB), SUB)
        irows = pl.ds(pl.multiple_of(block + r * SUB, SUB), SUB)

        def pair(ref, s):
            return ref[s, rows, :], ref[s, irows, :]

        if blocks <= UNROLL:
            left = [pair(spec_ref, c) for c in range(blocks)]
            right = [pair(joined_ref, c) for c in range(blocks)]
            for a in range(blocks):
                real, imag = conj_times(left[0], right[a])
                for c in range(1, blocks - a):
                    more = conj_times(left[c], right[a + c])
                    real, imag = real + more[0], imag + more[1]
                spec_ref[a, rows, :] = real
                spec_ref[a, irows, :] = imag
        else:

            def keep(c):
                hold_ref[c, :SUB, :], hold_ref[c, SUB:, :] = pair(spec_ref, c)

            def row(a):
                def term(c, sums):
                    left = hold_ref[c, :SUB, :], hold_ref[c, SUB:, :]
                    more = conj_times(left, pair(joined_ref, a + c))
                    return sums[0] + more[0], sums[1] + more[1]

                zero = jnp.zeros((SUB, lanes), F32)
                real, imag = lax.fori_loop(0, blocks - a, term, (zero, zero))
                spec_ref[a, rows, :] = real
                spec_ref[a, irows, :] = imag

            each(blocks, keep)
            each(blocks, row)
        return carry

    lax.fori_loop(0, block // SUB, chunk, 0)


def block_rows(ref, s, block):
    start = s * block
    if not isinstance(start, int):
        start = pl.multiple_of(start, block)
    return ref[pl.ds(start, block), :]


def set_rows(ref, s, block, value):
    start = s * block
    if not isinstance(start, int):
        start = pl.multiple_of(start, block)
    ref[pl.ds(start, block), :] = value


def long_kernel(scale, saved_ref, grad_ref, ftab_ref, itab_ref, medium_ref, out_ref, filt, prod, grad, hold):
    blocks, double, lanes = filt.shape
    block = double // 2
    height = saved_ref.shape[2]
    many = block // height

    def part(index, s):
        return saved_ref[pl.ds(s * many, many), index].reshape(block, lanes)

    def spread(s):
        product = (part(1, s).astype(F32) * part(2, s).astype(F32)).astype(BF16)
        spectrum = forward(ftab_ref, jnp.concatenate([part(0, s), product], axis=1))
        filt[s] = spectrum[:, :lanes]
        prod[s] = spectrum[:, lanes:]

    def spread_grad(s):
        value = [block_rows(grad_ref, 2 * s + half, block) for half in range(2)]
        spectrum = forward(ftab_ref, jnp.concatenate(value, axis=1))
        grad[2 * s] = spectrum[:, :lanes]
        grad[2 * s + 1] = spectrum[:, lanes:]

    def finish(a):
        time = inverse(itab_ref, jnp.concatenate([filt[a], prod[a]], axis=1), block) * scale
        point = time[:, :lanes]
        set_rows(medium_ref, a, block, (point * part(1, a).astype(F32)).astype(BF16))
        inner = (point * part(2, a).astype(F32)).astype(BF16)
        out_ref[pl.ds(a * many, many), 0] = inner.reshape(many, height, lanes)
        outer = time[:, lanes:].astype(BF16)
        out_ref[pl.ds(a * many, many), 1] = outer.reshape(many, height, lanes)

    each(blocks, spread)
    each(blocks // 2, spread_grad)
    join(grad)
    correlate(filt, grad, hold)
    correlate(prod, grad, hold)
    each(blocks, finish)


def short_kernel(
    scale,
    factor,
    grad_ref,
    saved_ref,
    medium_ref,
    short_ref,
    ftab_ref,
    itab_ref,
    out_ref,
    taps_ref,
    grad,
    saved,
    taps,
    tail,
):
    blocks, double, lanes = grad.shape
    block = double // 2
    height = saved_ref.shape[2]
    many = block // height
    medium = medium_ref.shape[0]
    short = short_ref.shape[0]
    total = blocks * block

    def spread(s):
        part = saved_ref[pl.ds(s * many, many), 3].reshape(block, lanes)
        value = jnp.concatenate([block_rows(grad_ref, s, block), part], axis=1)
        spectrum = forward(ftab_ref, value)
        grad[s] = spectrum[:, :lanes]
        saved[s] = spectrum[:, lanes:]

    each(blocks, spread)
    padded = jnp.concatenate([medium_ref[...], jnp.zeros((block - medium, lanes), BF16)], axis=0)
    taps[...] = forward(ftab_ref, padded)
    join(grad)

    def chunk(r, carry):
        rows = pl.ds(pl.multiple_of(r * SUB, SUB), SUB)
        irows = pl.ds(pl.multiple_of(block + r * SUB, SUB), SUB)
        tap = taps[rows, :], taps[irows, :]

        def term(s, sums):
            right = grad[s, rows, :], grad[s, irows, :]
            more = conj_times((saved[s, rows, :], saved[s, irows, :]), right)
            grad[s, rows, :], grad[s, irows, :] = conj_times(tap, right)
            return sums[0] + more[0], sums[1] + more[1]

        zero = jnp.zeros((SUB, lanes), F32)
        sums = (zero, zero)
        if blocks <= UNROLL:
            for s in range(blocks):
                sums = term(s, sums)
        else:
            sums = lax.fori_loop(0, blocks, term, sums)
        taps[rows, :], taps[irows, :] = sums
        return carry

    lax.fori_loop(0, block // SUB, chunk, 0)
    tap_grad = inverse(itab_ref, taps[...], block)[:medium] * (scale * factor)

    def finish(s):
        pair = jnp.concatenate([grad[2 * s], grad[2 * s + 1]], axis=1)
        time = inverse(itab_ref, pair, block) * scale
        for half in range(2):
            value = time[:, half * lanes : (half + 1) * lanes].astype(BF16).astype(F32)
            set_rows(tail, 2 * s + half, block, value)

    each(blocks // 2, finish)
    tail[total : total + 2 * SUB, :] = jnp.zeros((2 * SUB, lanes), F32)

    def span(b, sums):
        base = pl.multiple_of(b * height, height)
        values = saved_ref[b, 4].astype(F32)
        result = jnp.zeros((height, lanes), F32)
        new = []
        for j in range(short):
            shifted = tail[pl.ds(base + j, height), :]
            result = result + short_ref[j : j + 1, :].astype(F32) * shifted
            pieces = (values * shifted).reshape(height // SUB, SUB, lanes)
            new.append(sums[j] + jnp.sum(pieces, axis=0))
        out_ref[b] = result.astype(BF16)
        return tuple(new)

    start = tuple(jnp.zeros((SUB, lanes), F32) for _ in range(short))
    sums = lax.fori_loop(0, total // height, span, start)
    rows = [jnp.sum(value, axis=0, keepdims=True) * factor for value in sums]
    rest = taps_ref.shape[0] - medium
    rows.append(jnp.zeros((rest - short, lanes), F32))
    taps_ref[:medium, :] = tap_grad.astype(BF16)
    taps_ref[medium:, :] = jnp.concatenate(rows, axis=0).astype(BF16)


def call(kernel, outs, scratch, flops, *args):
    vmem = pl.BlockSpec(memory_space=pltpu.VMEM)
    return pl.pallas_call(
        kernel,
        out_shape=outs,
        in_specs=[vmem] * len(args),
        out_specs=jax.tree.map(lambda _: vmem, outs),
        scratch_shapes=scratch,
        compiler_params=pltpu.CompilerParams(vmem_limit_bytes=VMEM_LIMIT),
        cost_estimate=pl.CostEstimate(flops=flops, bytes_accessed=1 << 23, transcendentals=0),
    )(*args)


def pack_kernel(*refs):
    *ins, out_ref = refs
    outer, _, _, _, narrow = out_ref.shape
    for index, ref in enumerate(ins):
        for o in range(outer):
            out_ref[o, 0, index] = ref[:, o * narrow : (o + 1) * narrow]


def pack(values, outer, inner):
    height, channels = values[0].shape
    narrow = channels // (outer * inner)
    wide = channels // inner
    shape = (outer, inner, len(values), height, narrow)
    return pl.pallas_call(
        pack_kernel,
        out_shape=jax.ShapeDtypeStruct(shape, values[0].dtype),
        grid=(inner,),
        in_specs=[pl.BlockSpec((height, wide), lambda i: (0, i))] * len(values),
        out_specs=pl.BlockSpec((outer, 1) + shape[2:], lambda i: (0, i, 0, 0, 0)),
        cost_estimate=pl.CostEstimate(flops=1 << 28, bytes_accessed=1 << 22, transcendentals=0),
    )(*values)


def unpack_kernel(places, in_ref, *out_refs):
    _, outer, _, narrow = in_ref.shape
    for (start, count), out_ref in zip(places, out_refs):
        for o in range(outer):
            part = in_ref[0, o, start : start + count].astype(out_ref.dtype)
            out_ref[:, o * narrow : (o + 1) * narrow] = part


def unpack(value, order, *outs):
    inner, outer, length, narrow = value.shape
    wide = outer * narrow
    return pl.pallas_call(
        functools.partial(unpack_kernel, tuple(out[:2] for out in outs)),
        out_shape=[jax.ShapeDtypeStruct((count, wide * inner), kind) for _, count, kind in outs],
        grid=(inner,),
        in_specs=[pl.BlockSpec((1, outer, length, narrow), lambda i: (order(i), 0, 0, 0))],
        out_specs=[pl.BlockSpec((count, wide), lambda i: (0, i)) for _, count, _ in outs],
        cost_estimate=pl.CostEstimate(flops=1 << 28, bytes_accessed=1 << 22, transcendentals=0),
    )(value)


def unpack_devices(value, outer, inner, *outs):
    _, length, narrow = value.shape
    wide = outer * narrow

    def kernel(in_ref, *out_refs):
        for (start, count, _), out_ref in zip(outs, out_refs):
            for o in range(outer):
                part = in_ref[o, 0, start : start + count].astype(out_ref.dtype)
                out_ref[:, o * narrow : (o + 1) * narrow] = part

    return pl.pallas_call(
        kernel,
        out_shape=[jax.ShapeDtypeStruct((count, wide * inner), kind) for _, count, kind in outs],
        grid=(inner,),
        in_specs=[pl.BlockSpec((outer, 1, length, narrow), lambda i: (0, i, 0, 0))],
        out_specs=[pl.BlockSpec((count, wide), lambda i: (0, i)) for _, count, _ in outs],
        cost_estimate=pl.CostEstimate(flops=1 << 28, bytes_accessed=1 << 22, transcendentals=0),
    )(value.reshape(outer, inner, length, narrow))


def gather(value, axis):
    count = lax.axis_size(axis)
    place = lax.axis_index(axis)
    result = jnp.stack([value] * count)
    for step in range(1, count):
        more = lax.ppermute(value, axis, [(s, (s + step) % count) for s in range(count)])
        result = lax.dynamic_update_index_in_dim(result, more, (place - step) % count, 0)
    return result


def trade(value, axis, dim):
    count = lax.axis_size(axis)
    place = lax.axis_index(axis)
    result = value
    for step in range(1, count):
        sent = lax.dynamic_index_in_dim(value, (place + step) % count, dim, keepdims=True)
        got = lax.ppermute(sent, axis, [(s, (s + step) % count) for s in range(count)])
        result = lax.dynamic_update_slice_in_dim(result, got, (place - step) % count, dim)
    return result


def swap(value, axes):
    return lax.all_to_all(value, axes, split_axis=0, concat_axis=0, tiled=True)


def per_device(
    out_grad,
    out_weight,
    outer_gate,
    long_out,
    inner_gate,
    conv_input,
    short_out,
    medium_out,
    long_filter,
    taps_short,
    taps_medium,
):
    height, channels = outer_gate.shape
    halves, lines, pairs, cores = (lax.axis_size(axis) for axis in ("h", "l", "j", "k"))
    groups = lax.axis_size("ch")
    outer = halves * lines
    inner = pairs * cores
    devices = outer * inner
    total = height * devices
    narrow = channels // devices
    wide = channels // inner
    medium, short = taps_medium.shape[0], taps_short.shape[0]
    planes = ("h", "l")
    seq = planes + ("j", "k")
    half, line = lax.axis_index("h"), lax.axis_index("l")
    me = half * lines + line
    my_inner = lax.axis_index("j") * cores + lax.axis_index("k")

    saved = pack([long_filter, inner_gate, medium_out, short_out, conv_input], outer, inner)
    saved = swap(saved.reshape((devices,) + saved.shape[2:]), seq)

    rows = out_weight.shape[0]
    depth = inner * groups * rows

    def to_columns(value):
        value = value.reshape(rows, groups, pairs, cores, wide).transpose(2, 3, 1, 0, 4)
        for axis, dim in (("j", 0), ("ch", 2), ("k", 1)):
            value = trade(value, axis, dim)
        return value.reshape(depth, wide)

    blocks = [(to_columns(out_weight), line)]
    for step in range(1, lines):
        shift = [(s, (s + step) % lines) for s in range(lines)]
        more = lax.ppermute(out_weight, "l", shift)
        blocks.append((to_columns(more), (line - step) % lines))

    both = gather(out_grad, "ch")
    share = height // groups
    first = lax.axis_index("ch") * share
    piece = lax.dynamic_slice(both, (1 - half, first, 0), (1, share, channels))
    piece = lax.ppermute(piece[0], "h", [(0, 1), (1, 0)])
    piece = gather(piece, "ch").reshape(height, channels)
    mine = lax.dynamic_index_in_dim(both, half, 0, keepdims=False)
    mine = gather(gather(mine, "j"), "k")
    mine = mine.reshape(inner * height, channels)
    other = gather(gather(piece, "j"), "k")
    other = other.reshape(inner * height, channels)

    def term(value, block, source):
        return dot(lax.dynamic_slice_in_dim(value, source * depth, depth, 1), block)

    away = sum(term(other, block, source) for block, source in blocks).astype(BF16)
    away = lax.ppermute(away, "h", [(0, 1), (1, 0)])
    hidden = sum(term(mine, block, source) for block, source in blocks) + away.astype(F32)
    hidden = hidden.reshape(cores, pairs, height, wide).transpose(1, 0, 2, 3)

    def to_plane(value):
        return value.reshape(height, pairs, cores, wide).transpose(1, 2, 0, 3)

    gates = jnp.stack([to_plane(outer_gate), to_plane(long_out)], axis=2)
    gates = trade(trade(gates, "j", 0), "k", 1).astype(F32)
    long_grad = (hidden * gates[:, :, 0]).astype(BF16).reshape(inner * height, outer, narrow)
    long_grad, saved = lax.optimization_barrier((long_grad.transpose(1, 0, 2), saved))
    long_grad = swap(long_grad, planes).reshape(total, narrow)
    grad_outer = (hidden * gates[:, :, 1]).astype(BF16)
    grad_outer = trade(trade(grad_outer, "j", 0), "k", 1)
    grad_outer = grad_outer.transpose(2, 0, 1, 3).reshape(height, channels)

    first = (my_inner * outer + me) * narrow
    my_medium = lax.dynamic_slice_in_dim(taps_medium, first, narrow, 1)
    my_short = lax.dynamic_slice_in_dim(taps_short, first, narrow, 1)

    saved = jnp.pad(saved, [(0, 0)] * 3 + [(0, -narrow % LANES)])
    lanes = -(-narrow // LANES) * LANES

    def pad(value):
        return jnp.pad(value, [(0, 0)] * (value.ndim - 1) + [(0, lanes - narrow)])

    block = max(height, min(BLOCK, total // 2))
    blocks = total // block
    high, low = table(block)
    ftab = jnp.concatenate([high, low])
    itab = jnp.concatenate([high.T, low.T])
    factor = total ** (-0.5)
    spectra = pltpu.VMEM((blocks, 2 * block, lanes), F32)
    hold = pltpu.VMEM((blocks, 2 * SUB, lanes), F32)
    out = jax.ShapeDtypeStruct
    medium_grad, sent_long = call(
        functools.partial(long_kernel, factor / block),
        (out((total, lanes), BF16), out((devices, 2, height, lanes), BF16)),
        [spectra] * 3 + [hold],
        24 * 2 * block * total * lanes,
        saved,
        pad(long_grad),
        ftab,
        itab,
    )
    rest = -(-short // 16) * 16
    sent_short, tap_grads = call(
        functools.partial(short_kernel, 1.0 / block, factor),
        (out((devices, height, lanes), BF16), out((medium + rest, lanes), BF16)),
        [spectra] * 2
        + [pltpu.VMEM((2 * block, lanes), F32), pltpu.VMEM((total + 2 * SUB, lanes), F32)],
        16 * 2 * block * total * lanes,
        medium_grad,
        saved,
        pad(my_medium),
        pad(my_short),
        ftab,
        itab,
    )
    sent_long = sent_long.reshape(devices, 2 * height, lanes)
    got_long = swap(sent_long[..., :narrow], seq)
    tap_grads = tap_grads[:, :narrow]
    for axis in ("l", "h", "j", "k"):
        tap_grads = gather(tap_grads, axis)
    got_long, sent_short = lax.optimization_barrier((got_long, sent_short))
    grad_inner, grad_filter = unpack_devices(
        got_long, outer, inner, (0, height, BF16), (height, height, F32)
    )
    got_short = swap(sent_short[..., :narrow], seq)
    (grad_input,) = unpack_devices(got_short, outer, inner, (0, height, BF16))
    grad_medium, grad_short = unpack(
        tap_grads.reshape(inner, outer, -1, narrow),
        lambda i: i % cores * pairs + i // cores,
        (0, medium, F32),
        (medium, short, F32),
    )
    return grad_outer, grad_inner, grad_input, grad_filter, grad_short, grad_medium


def solution(mesh):
    devices, groups = mesh.shape["seq"], mesh.shape["ch"]
    inner = 2 ** ((devices.bit_length() - 1) // 2)
    cores = min(2, inner)
    fine = Mesh(
        mesh.devices.reshape(2, devices // inner // 2, inner // cores, cores, groups),
        ("h", "l", "j", "k", "ch"),
    )
    seq = ("h", "l", "j", "k")
    tokens = P(seq, "ch")
    taps = P(None, "ch")

    return jax.shard_map(
        per_device,
        mesh=fine,
        in_specs=(tokens, P(seq + ("ch",), None)) + (tokens,) * 7 + (taps, taps),
        out_specs=(tokens,) * 4 + (taps, taps),
        check_vma=False,
    )
```

time: 593 us -> 277 us (0.47); the launches traced: 585 us -> 275 us
  matrix products: 200 us -> 4.21 us
  blocking collectives: 93 us -> 0 us
  local copies, waits for them, and re-layouts: 73.2 us -> 29.9 us
  Pallas kernels: 0 us -> 32.9 us
  between operations: 15.2 us -> 1.23 us
    dot_general x71 -> x4, matrix products: 168 us -> 4.21 us  [dot(): return jnp.dot(left, right, preferred_element_type=F32)]
    ppermute x4 -> x23, waiting for transfers between devices: 0.85 us -> 135 us  [the longest x1 56.8 us: per_device(): piece = lax.ppermute(piece[0], 'h', [(0, 1), (1, 0)])]
    psum x1 -> x0, blocking collectives: 68.9 us -> none  [per_device(): sum_medium, sum_short = lax.psum((partial_medium, partial_short), 'seq')]
    all_gather x2 -> x0, waiting for transfers between devices: 56.4 us -> none  [the longest x1 56.4 us: per_device(): lax.all_gather(aligned, 'seq', axis=0, tiled=True)]
    all_to_all x4, waiting for transfers between devices: 65.8 us -> 10.3 us  [swap(): return lax.all_to_all(value, axes, split_axis=0, concat_axis=0, tiled=True)]
    conv_general_dilated x4 -> x0, matrix products: 32.9 us -> none  [depthwise(): lax.conv_general_dilated(signal.astype(jnp.float32)[None], kernel.astype(...]
    pallas_call x0 -> x6, Pallas kernels: none -> 32.9 us  [the longest x2 18.7 us: call(): pl.pallas_call(kernel, out_shape=outs, in_specs=[vmem] * len(args), out_s...]
    unnamed x135 -> x25, local copies, waits for them, and re-layouts: 31.9 us -> 5.64 us
  transfers between devices with their start and end apart: 11 -> 27, of which waited for: 6 -> 11; matrix products, arithmetic and copies ran while one was open for 19% -> 18% of each run, Pallas kernels for 0% -> 7%
where the time goes in v1:
time: 277 us; the launch traced here: 275 us
  waiting for transfers between devices  145 us (52%)
  starting transfers between devices  42 us (15%)
  Pallas kernels  32.9 us (12%)
  local copies, waits for them, and re-layouts  29.9 us (11%)
  other arithmetic  20.1 us (7%)
  matrix products  4.21 us (2%)
    ppermute x1, waiting for transfers between devices, per_device(): piece = lax.ppermute(piece[0], 'h', [(0, 1), (1, 0)])  56.8 us
    ppermute x10, waiting for transfers between devices, trade(): lax.ppermute(sent, axis, [(s, (s + step) % count) for s in range(count)])  43.3 us
    ppermute x1, waiting for transfers between devices, per_device(): away = lax.ppermute(away, 'h', [(0, 1), (1, 0)])  22.5 us
    pallas_call x2, Pallas kernels, call(): pl.pallas_call(kernel, out_shape=outs, in_specs=[vmem] * len(args), out_s...  18.7 us
    all_to_all x4, starting transfers between devices, swap(): return lax.all_to_all(value, axes, split_axis=0, concat_axis=0, tiled=True)  18 us
    ppermute x10, starting transfers between devices, gather(): lax.ppermute(value, axis, [(s, (s + step) % count) for s in range(count)])  12.7 us
    ppermute x10, waiting for transfers between devices, gather(): lax.ppermute(value, axis, [(s, (s + step) % count) for s in range(count)])  12 us
    all_to_all x4, waiting for transfers between devices, swap(): return lax.all_to_all(value, axes, split_axis=0, concat_axis=0, tiled=True)  10.3 us
  transfers between devices with their start and end apart: 27, of which 11 were waited for; matrix products, arithmetic and copies ran while one was open for 18% of the time, Pallas kernels for 7%

profile of v1, /device:TPU:0, one launch (start us, length us, event | category | flops | bytes accessed | tf_op | source)
XLA Modules:
  0.0 275.3 jit_solution(6847962041908377777)
XLA Ops:
  0.7 3.1 %collective-permute-start = (bf16[128,2048]{1,0:T(8,128)(2,1)}, bf16[128,2048]{1,0:T(8,128)(2,1)}, u32[]{:S(2)}, u32[]{:S(2)}) collective-permute-start(bf16[128,2048]{1,0:T(8,128)(2,1)} %param.11), channel_id=1, source_target_pairs={{0,1},{1,0},{2,3},{3,2},{4,5},{5,4},{6,7},{7,6},{8,9},{9,8},{10,11... | collective-permute-start | bytes 1572872 | tf_op jit(solution)/shard_map/ppermute | solution.py:358
  10.5 2.2 reshape.111
  16.3 4.2 %shard_map.154 = bf16[4,4,5,128,128]{4,3,2,1,0:T(8,128)(2,1)} custom-call(bf16[128,2048]{1,0:T(8,128)(2,1)} %refs_0_.1, bf16[128,2048]{1,0:T(8,128)(2,1)} %refs_1_.1, bf16[128,2048]{1,0:T(8,128)(2,1)} %refs_2_.1, bf16[128,2048]{1,0:T(8,128)(2,1)} %refs_3_.1, bf16[128,2048]{1,0:T(8,128)(2,1)} %refs_4_.1), custom_call_target="tpu_custom_call" | custom-call | flops 268435456 | bytes 4194304 | tf_op jit(solution)/shard_map/pallas_call | solution.py:302
  20.5 4.9 %all-to-all-start = ((bf16[16,5,128,128]{3,2,1,0:T(8,128)(2,1)}), bf16[16,5,128,128]{3,2,1,0:T(8,128)(2,1)}, u32[]{:S(2)}, u32[]{:S(2)}) async-start(bf16[16,5,128,128]{3,2,1,0:T(8,128)(2,1)} %bitcast.88), calls=%async_computation | async-start | bytes 5242880 | tf_op jit(solution)/shard_map/all_to_all | solution.py:375
  28.0 2.7 collective-permute-start.10
  32.4 5.6 %collective-permute-done.15 = bf16[1,2,2,128,512]{4,3,1,0,2:T(8,128)(2,1)} collective-permute-done((bf16[1,2,2,128,512]{4,3,1,0,2:T(8,128)(2,1)}, bf16[1,2,2,128,512]{4,3,1,0,2:T(8,128)(2,1)}, u32[]{:S(2)}, u32[]{:S(2)}) %collective-permute-start.15) | collective-permute-done | bytes 524320 | tf_op jit(solution)/shard_map/ppermute | solution.py:369
  40.1 56.8 %collective-permute-done.10 = bf16[64,2048]{1,0:T(8,128)(2,1)S(1)} collective-permute-done((bf16[64,2048]{1,0:T(8,128)(2,1)S(1)}, bf16[64,2048]{1,0:T(8,128)(2,1)S(1)}, u32[]{:S(2)}, u32[]{:S(2)}) %collective-permute-start.10) | collective-permute-done | bytes 262176 | tf_op jit(solution)/shard_map/ppermute | solution.py:429
  97.6 7.1 %collective-permute-done.11 = bf16[64,2048]{1,0:T(8,128)(2,1)S(1)} collective-permute-done((bf16[64,2048]{1,0:T(8,128)(2,1)S(1)}, bf16[64,2048]{1,0:T(8,128)(2,1)S(1)}, u32[]{:S(2)}, u32[]{:S(2)}) %collective-permute-start.11) | collective-permute-done | bytes 262176 | tf_op jit(solution)/shard_map/ppermute | solution.py:358
  110.5 3.1 %pad_maximum_fusion = bf16[2,2,128,2048]{3,2,1,0:T(8,128)(2,1)} fusion(bf16[1,2,128,2048]{3,2,1,0:T(8,128)(2,1)} %bitcast.4), kind=kLoop, calls=%fused_computation | loop fusion | flops 1048576 | bytes 3145728 | tf_op jit(solution)/shard_map/stack | solution.py:356
  113.6 14.9 %collective-permute-done.7 = bf16[1,2,2,128,512]{3,4,1,0,2:T(8,128)(2,1)S(1)} collective-permute-done((bf16[1,2,2,128,512]{3,4,1,0,2:T(8,128)(2,1)S(1)}, bf16[1,2,2,128,512]{3,4,1,0,2:T(8,128)(2,1)S(1)}, u32[]{:S(2)}, u32[]{:S(2)}) %collective-permute-start.7) | collective-permute-done | bytes 524320 | tf_op jit(solution)/shard_map/ppermute | solution.py:369
  130.7 9.6 %collective-permute-done.8 = bf16[2,2,1,128,512]{3,4,1,0,2:T(8,128)(2,1)S(1)} collective-permute-done((bf16[2,2,1,128,512]{3,4,1,0,2:T(8,128)(2,1)S(1)}, bf16[2,2,1,128,512]{3,4,1,0,2:T(8,128)(2,1)S(1)}, u32[]{:S(2)}, u32[]{:S(2)}) %collective-permute-start.8) | collective-permute-done | bytes 524320 | tf_op jit(solution)/shard_map/ppermute | solution.py:369
  143.0 3.0 %pad_maximum_fusion.1 = bf16[2,2,128,2048]{3,2,1,0:T(8,128)(2,1)} fusion(bf16[1,2,128,2048]{3,2,1,0:T(8,128)(2,1)} %bitcast.21), kind=kLoop, calls=%fused_computation.1 | loop fusion | flops 1048576 | bytes 3145728 | tf_op jit(solution)/shard_map/stack | solution.py:356
  148.0 2.3 bitcast_dynamic-update-slice_fusion
  150.3 2.1 fusion.6
  156.1 22.5 %collective-permute-done.14 = bf16[512,512]{1,0:T(8,128)(2,1)S(1)} collective-permute-done((bf16[512,512]{1,0:T(8,128)(2,1)S(1)}, bf16[512,512]{1,0:T(8,128)(2,1)S(1)}, u32[]{:S(2)}, u32[]{:S(2)}) %collective-permute-start.14) | collective-permute-done | bytes 524320 | tf_op jit(solution)/shard_map/ppermute | solution.py:441
  180.8 3.7 %all-to-all-start.1 = ((bf16[4,512,128]{2,1,0:T(8,128)(2,1)}), bf16[4,512,128]{2,1,0:T(8,128)(2,1)S(1)}, u32[]{:S(2)}, u32[]{:S(2)}) async-start(bf16[4,512,128]{2,1,0:T(8,128)(2,1)} %copy.42), calls=%async_computation.1 | async-start | bytes 1048576 | tf_op jit(solution)/shard_map/all_to_all | solution.py:375
  184.5 2.6 reduce-precision_convert_fusion.1
  188.0 2.3 reduce-precision_convert_fusion
  191.1 8.2 %all-to-all-done.1 = bf16[4,512,128]{2,1,0:T(8,128)(2,1)S(1)} async-done(((bf16[4,512,128]{2,1,0:T(8,128)(2,1)}), bf16[4,512,128]{2,1,0:T(8,128)(2,1)S(1)}, u32[]{:S(2)}, u32[]{:S(2)}) %all-to-all-start.1) | async-done | bytes 524320 | tf_op jit(solution)/shard_map/all_to_all | solution.py:375
  200.1 10.5 %shard_map.155 = (bf16[2048,128]{1,0:T(8,128)(2,1)}, bf16[16,2,128,128]{3,2,1,0:T(8,128)(2,1)}) custom-call(bf16[16,5,128,128]{3,2,1,0:T(8,128)(2,1)} %all-to-all-done.saved_ref, bf16[2048,128]{1,0:T(8,128)(2,1)} %bitcast.111, bf16[1024,256]{1,0:T(8,128)(2,1)} %pad_maximum_fusion.8.ftab_ref, bf16[512,512]{1,0:T(8,128)(2,1)} %pad_maximum_fusion.9.itab_ref), custom_call_target="tpu_custom_call" | custom-call | flops 3221225472 | bytes 8388608 | tf_op jit(solution)/shard_map/pallas_call | solution.py:278
  210.6 3.7 %all-to-all-start.2 = ((bf16[16,256,128]{2,1,0:T(8,128)(2,1)}), bf16[16,256,128]{2,1,0:T(8,128)(2,1)S(1)}, u32[]{:S(2)}, u32[]{:S(2)}) async-start(bf16[16,256,128]{2,1,0:T(8,128)(2,1)} %bitcast.105), calls=%async_computation.2 | async-start | bytes 2097152 | tf_op jit(solution)/shard_map/all_to_all | solution.py:375
  214.4 2.0 collective-permute-start.17
  218.2 13.2 %collective-permute-done.17 = bf16[1,2,128,512]{3,2,1,0:T(8,128)(2,1)S(1)} collective-permute-done((bf16[1,2,128,512]{3,2,1,0:T(8,128)(2,1)S(1)}, bf16[1,2,128,512]{3,2,1,0:T(8,128)(2,1)S(1)}, u32[]{:S(2)}, u32[]{:S(2)}) %collective-permute-start.17) | collective-permute-done | bytes 262176 | tf_op jit(solution)/shard_map/ppermute | solution.py:369
  231.5 8.2 %shard_map.156 = (bf16[16,128,128]{2,1,0:T(8,128)(2,1)}, bf16[144,128]{1,0:T(8,128)(2,1)}) custom-call(bf16[2048,128]{1,0:T(8,128)(2,1)} %get-tuple-element.21.grad_ref, bf16[16,5,128,128]{3,2,1,0:T(8,128)(2,1)} %all-to-all-done.saved_ref, bf16[128,128]{1,0:T(8,128)(2,1)} %constant_dynamic-slice_fusion.1.medium_ref, ...), custom_call_target="tpu_custom_call" | custom-call | flops 2147483648 | bytes 8388608 | tf_op jit(solution)/shard_map/pallas_call | solution.py:278
  241.3 2.6 collective-permute-done.19
  243.8 3.3 %collective-permute-start.20 = (bf16[2,144,128]{2,1,0:T(8,128)(2,1)S(1)}, bf16[2,144,128]{2,1,0:T(8,128)(2,1)S(1)}, u32[]{:S(2)}, u32[]{:S(2)}) collective-permute-start(bf16[2,144,128]{2,1,0:T(8,128)(2,1)S(1)} %bitcast_dynamic-update-slice_fusion.9), channel_id=1, source_target_pairs={{0,16},{16,0},{1,17},{17,1},{2,18},{18,2},{3,19},{19,3},{4,20},{20... | collective-permute-start | bytes 221192 | tf_op jit(solution)/shard_map/ppermute | solution.py:358
  247.1 2.3 collective-permute-done.20
  251.3 5.7 %all-to-all-start.3 = ((bf16[16,128,128]{2,1,0:T(8,128)(2,1)}), bf16[16,128,128]{2,1,0:T(8,128)(2,1)S(1)}, u32[]{:S(2)}, u32[]{:S(2)}) async-start(bf16[16,128,128]{2,1,0:T(8,128)(2,1)} %get-tuple-element.25), calls=%async_computation.3 | async-start | bytes 1048576 | tf_op jit(solution)/shard_map/all_to_all | solution.py:375
  262.3 3.3 %shard_map.159 = (f32[128,2048]{1,0:T(8,128)}, f32[7,2048]{1,0:T(8,128)}) custom-call(bf16[4,4,144,128]{3,2,1,0:T(8,128)(2,1)} %bitcast.109), custom_call_target="tpu_custom_call" | custom-call | flops 268435456 | bytes 4194304 | tf_op jit(solution)/shard_map/pallas_call | solution.py:323
  265.6 3.5 %shard_map.157 = (bf16[128,2048]{1,0:T(8,128)(2,1)}, f32[128,2048]{1,0:T(8,128)}) custom-call(bf16[4,4,256,128]{3,2,1,0:T(8,128)(2,1)} %bitcast.96), custom_call_target="tpu_custom_call" | custom-call | flops 268435456 | bytes 4194304 | tf_op jit(solution)/shard_map/pallas_call | solution.py:343
  269.1 2.1 all-to-all-done.3
  272.1 3.2 %shard_map.158 = bf16[128,2048]{1,0:T(8,128)(2,1)} custom-call(bf16[4,4,128,128]{3,2,1,0:T(8,128)(2,1)} %bitcast.102), custom_call_target="tpu_custom_call" | custom-call | flops 268435456 | bytes 4194304 | tf_op jit(solution)/shard_map/pallas_call | solution.py:343
  (120 shorter events, 49.6 us)
Async XLA Ops:
  0.6 217.0 %copy-start = (bf16[128,2048]{1,0:T(8,128)(2,1)S(1)}, bf16[128,2048]{1,0:T(8,128)(2,1)}, u32[]{:S(2)}) copy-start(bf16[128,2048]{1,0:T(8,128)(2,1)} %param.21) | copy-start | bytes 1572868
  0.6 8.7 %copy-start.10 = (bf16[128,2048]{1,0:T(8,128)(2,1)S(1)}, bf16[128,2048]{1,0:T(8,128)(2,1)}, u32[]{:S(2)}) copy-start(bf16[128,2048]{1,0:T(8,128)(2,1)} %param.13) | copy-start | bytes 1572868
  0.7 26.2 %collective-permute-start = (bf16[128,2048]{1,0:T(8,128)(2,1)}, bf16[128,2048]{1,0:T(8,128)(2,1)}, u32[]{:S(2)}, u32[]{:S(2)}) collective-permute-start(bf16[128,2048]{1,0:T(8,128)(2,1)} %param.11), channel_id=1, source_target_pairs={{0,1},{1,0},{2,3},{3,2},{4,5},{5,4},{6,7},{7,6},{8,9},{9,8},{10,11... | collective-permute-start | bytes 1572872 | tf_op jit(solution)/shard_map/ppermute | solution.py:358
  5.3 100.9 %collective-permute-start.6 = (bf16[128,4096]{0,1:T(8,128)(2,1)S(1)}, bf16[128,4096]{0,1:T(8,128)(2,1)S(1)}, u32[]{:S(2)}, u32[]{:S(2)}) collective-permute-start(bf16[128,4096]{0,1:T(8,128)(2,1)S(1)} %copy.34), channel_id=1, source_target_pairs={{0,8},{8,0},{1,9},{9,1},{2,10},{10,2},{3,11},{11,3},{4,12},{12,4},... | collective-permute-start | bytes 3145736 | tf_op jit(solution)/shard_map/ppermute | solution.py:422
  7.8 99.1 %collective-permute-start.3 = (bf16[1,2,2,128,512]{3,4,1,0,2:T(8,128)(2,1)}, bf16[1,2,2,128,512]{3,4,1,0,2:T(8,128)(2,1)}, u32[]{:S(2)}, u32[]{:S(2)}) collective-permute-start(bf16[1,2,2,128,512]{3,4,1,0,2:T(8,128)(2,1)} %dynamic-slice_bitcast_fusion.1), channel_id=1, source_target_pairs={{0,4},{4,0},{1,5},{5,1},{2,6},{6,2},{3,7},{7,3},{8,12},{12,8},{9,1... | collective-permute-start | bytes 1572872 | tf_op jit(solution)/shard_map/ppermute | solution.py:369
  15.7 22.2 %collective-permute-start.15 = (bf16[1,2,2,128,512]{4,3,1,0,2:T(8,128)(2,1)}, bf16[1,2,2,128,512]{4,3,1,0,2:T(8,128)(2,1)}, u32[]{:S(2)}, u32[]{:S(2)}) collective-permute-start(bf16[1,2,2,128,512]{4,3,1,0,2:T(8,128)(2,1)} %fusion.20), channel_id=1, source_target_pairs={{0,4},{4,0},{1,5},{5,1},{2,6},{6,2},{3,7},{7,3},{8,12},{12,8},{9,1... | collective-permute-start | bytes 1572872 | tf_op jit(solution)/shard_map/ppermute | solution.py:369
  20.5 159.4 %all-to-all-start = ((bf16[16,5,128,128]{3,2,1,0:T(8,128)(2,1)}), bf16[16,5,128,128]{3,2,1,0:T(8,128)(2,1)}, u32[]{:S(2)}, u32[]{:S(2)}) async-start(bf16[16,5,128,128]{3,2,1,0:T(8,128)(2,1)} %bitcast.88), calls=%async_computation | async-start | bytes 5242880 | tf_op jit(solution)/shard_map/all_to_all | solution.py:375
  28.0 68.9 %collective-permute-start.10 = (bf16[64,2048]{1,0:T(8,128)(2,1)S(1)}, bf16[64,2048]{1,0:T(8,128)(2,1)S(1)}, u32[]{:S(2)}, u32[]{:S(2)}) collective-permute-start(bf16[64,2048]{1,0:T(8,128)(2,1)S(1)} %dynamic-slice_bitcast_fusion.2), channel_id=1, source_target_pairs={{0,16},{16,0},{1,17},{17,1},{2,18},{18,2},{3,19},{19,3},{4,20},{20... | collective-permute-start | bytes 786440 | tf_op jit(solution)/shard_map/ppermute | solution.py:429
  30.8 77.8 %collective-permute-start.1 = (bf16[128,2048]{1,0:T(8,128)(2,1)S(1)}, bf16[128,2048]{1,0:T(8,128)(2,1)S(1)}, u32[]{:S(2)}, u32[]{:S(2)}) collective-permute-start(bf16[128,2048]{1,0:T(8,128)(2,1)S(1)} %fusion.39), channel_id=1, source_target_pairs={{0,4},{4,0},{1,5},{5,1},{2,6},{6,2},{3,7},{7,3},{8,12},{12,8},{9,1... | collective-permute-start | bytes 1572872 | tf_op jit(solution)/shard_map/ppermute | solution.py:358
  96.9 7.8 %collective-permute-start.11 = (bf16[64,2048]{1,0:T(8,128)(2,1)S(1)}, bf16[64,2048]{1,0:T(8,128)(2,1)S(1)}, u32[]{:S(2)}, u32[]{:S(2)}) collective-permute-start(bf16[64,2048]{1,0:T(8,128)(2,1)S(1)} %collective-permute-done.10), channel_id=1, source_target_pairs={{0,1},{1,0},{2,3},{3,2},{4,5},{5,4},{6,7},{7,6},{8,9},{9,8},{10,11... | collective-permute-start | bytes 786440 | tf_op jit(solution)/shard_map/ppermute | solution.py:358
  97.4 43.8 %collective-permute-start.16 = (bf16[2,1,2,128,512]{4,3,1,0,2:T(8,128)(2,1)S(1)}, bf16[2,1,2,128,512]{4,3,1,0,2:T(8,128)(2,1)S(1)}, u32[]{:S(2)}, u32[]{:S(2)}) collective-permute-start(bf16[2,1,2,128,512]{4,3,1,0,2:T(8,128)(2,1)S(1)} %constant_dynamic-slice_fusion.4), channel_id=1, source_target_pairs={{0,2},{2,0},{1,3},{3,1},{4,6},{6,4},{5,7},{7,5},{8,10},{10,8},{9,1... | collective-permute-start | bytes 1572872 | tf_op jit(solution)/shard_map/ppermute | solution.py:369
  104.7 24.5 %collective-permute-start.12 = (bf16[128,2048]{1,0:T(8,128)(2,1)S(1)}, bf16[128,2048]{1,0:T(8,128)(2,1)S(1)}, u32[]{:S(2)}, u32[]{:S(2)}) collective-permute-start(bf16[128,2048]{1,0:T(8,128)(2,1)S(1)} %bitcast.98), channel_id=1, source_target_pairs={{0,4},{4,0},{1,5},{5,1},{2,6},{6,2},{3,7},{7,3},{8,12},{12,8},{9,1... | collective-permute-start | bytes 1572872 | tf_op jit(solution)/shard_map/ppermute | solution.py:358
  106.2 22.2 %collective-permute-start.7 = (bf16[1,2,2,128,512]{3,4,1,0,2:T(8,128)(2,1)S(1)}, bf16[1,2,2,128,512]{3,4,1,0,2:T(8,128)(2,1)S(1)}, u32[]{:S(2)}, u32[]{:S(2)}) collective-permute-start(bf16[1,2,2,128,512]{3,4,1,0,2:T(8,128)(2,1)S(1)} %dynamic-slice_bitcast_fusion), channel_id=1, source_target_pairs={{0,4},{4,0},{1,5},{5,1},{2,6},{6,2},{3,7},{7,3},{8,12},{12,8},{9,1... | collective-permute-start | bytes 1572872 | tf_op jit(solution)/shard_map/ppermute | solution.py:369
  108.0 22.0 %collective-permute-start.4 = (bf16[2,2,1,128,512]{3,4,1,0,2:T(8,128)(2,1)S(1)}, bf16[2,2,1,128,512]{3,4,1,0,2:T(8,128)(2,1)S(1)}, u32[]{:S(2)}, u32[]{:S(2)}) collective-permute-start(bf16[2,2,1,128,512]{3,4,1,0,2:T(8,128)(2,1)S(1)} %constant_dynamic-slice_fusion.8), channel_id=1, source_target_pairs={{0,1},{1,0},{2,3},{3,2},{4,5},{5,4},{6,7},{7,6},{8,9},{9,8},{10,11... | collective-permute-start | bytes 1572872 | tf_op jit(solution)/shard_map/ppermute | solution.py:369
  109.4 43.9 %collective-permute-start.2 = (bf16[2,128,2048]{2,1,0:T(8,128)(2,1)}, bf16[2,128,2048]{2,1,0:T(8,128)(2,1)}, u32[]{:S(2)}, u32[]{:S(2)}) collective-permute-start(bf16[2,128,2048]{2,1,0:T(8,128)(2,1)} %bitcast_dynamic-update-slice_fusion.3), channel_id=1, source_target_pairs={{0,2},{2,0},{1,3},{3,1},{4,6},{6,4},{5,7},{7,5},{8,10},{10,8},{9,1... | collective-permute-start | bytes 3145736 | tf_op jit(solution)/shard_map/ppermute | solution.py:358
  128.6 11.7 %collective-permute-start.8 = (bf16[2,2,1,128,512]{3,4,1,0,2:T(8,128)(2,1)S(1)}, bf16[2,2,1,128,512]{3,4,1,0,2:T(8,128)(2,1)S(1)}, u32[]{:S(2)}, u32[]{:S(2)}) collective-permute-start(bf16[2,2,1,128,512]{3,4,1,0,2:T(8,128)(2,1)S(1)} %constant_dynamic-slice_fusion.6), channel_id=1, source_target_pairs={{0,1},{1,0},{2,3},{3,2},{4,5},{5,4},{6,7},{7,6},{8,9},{9,8},{10,11... | collective-permute-start | bytes 1572872 | tf_op jit(solution)/shard_map/ppermute | solution.py:369
  130.0 18.0 %collective-permute-start.13 = (bf16[2,128,2048]{2,1,0:T(8,128)(2,1)}, bf16[2,128,2048]{2,1,0:T(8,128)(2,1)}, u32[]{:S(2)}, u32[]{:S(2)}) collective-permute-start(bf16[2,128,2048]{2,1,0:T(8,128)(2,1)} %bitcast_dynamic-update-slice_fusion.2), channel_id=1, source_target_pairs={{0,2},{2,0},{1,3},{3,1},{4,6},{6,4},{5,7},{7,5},{8,10},{10,8},{9,1... | collective-permute-start | bytes 3145736 | tf_op jit(solution)/shard_map/ppermute | solution.py:358
  130.1 15.9 %collective-permute-start.5 = (bf16[2,1,2,128,512]{3,4,1,0,2:T(8,128)(2,1)S(1)}, bf16[2,1,2,128,512]{3,4,1,0,2:T(8,128)(2,1)S(1)}, u32[]{:S(2)}, u32[]{:S(2)}) collective-permute-start(bf16[2,1,2,128,512]{3,4,1,0,2:T(8,128)(2,1)S(1)} %constant_dynamic-slice_fusion.7), channel_id=1, source_target_pairs={{0,2},{2,0},{1,3},{3,1},{4,6},{6,4},{5,7},{7,5},{8,10},{10,8},{9,1... | collective-permute-start | bytes 1572872 | tf_op jit(solution)/shard_map/ppermute | solution.py:369
  141.2 6.2 %collective-permute-start.9 = (bf16[2,1,2,128,512]{3,4,1,0,2:T(8,128)(2,1)}, bf16[2,1,2,128,512]{3,4,1,0,2:T(8,128)(2,1)S(1)}, u32[]{:S(2)}, u32[]{:S(2)}) collective-permute-start(bf16[2,1,2,128,512]{3,4,1,0,2:T(8,128)(2,1)} %constant_dynamic-slice_fusion.5), channel_id=1, source_target_pairs={{0,2},{2,0},{1,3},{3,1},{4,6},{6,4},{5,7},{7,5},{8,10},{10,8},{9,1... | collective-permute-start | bytes 1572872 | tf_op jit(solution)/shard_map/ppermute | solution.py:369
  150.3 2.2 copy-start.6
  153.3 25.4 %collective-permute-start.14 = (bf16[512,512]{1,0:T(8,128)(2,1)S(1)}, bf16[512,512]{1,0:T(8,128)(2,1)S(1)}, u32[]{:S(2)}, u32[]{:S(2)}) collective-permute-start(bf16[512,512]{1,0:T(8,128)(2,1)S(1)} %fusion.1), channel_id=1, source_target_pairs={{0,16},{16,0},{1,17},{17,1},{2,18},{18,2},{3,19},{19,3},{4,20},{20... | collective-permute-start | bytes 1572872 | tf_op jit(solution)/shard_map/ppermute | solution.py:441
  156.1 23.2 %copy-start.1 = (f32[2,2,2,128,512]{4,3,1,0,2:T(8,128)S(1)}, f32[2,2,2,128,512]{4,3,1,0,2:T(8,128)}, u32[]{:S(2)}) copy-start(f32[2,2,2,128,512]{4,3,1,0,2:T(8,128)} %convert_element_type.40) | copy-start | bytes 6291460
  180.8 18.5 %all-to-all-start.1 = ((bf16[4,512,128]{2,1,0:T(8,128)(2,1)}), bf16[4,512,128]{2,1,0:T(8,128)(2,1)S(1)}, u32[]{:S(2)}, u32[]{:S(2)}) async-start(bf16[4,512,128]{2,1,0:T(8,128)(2,1)} %copy.42), calls=%async_computation.1 | async-start | bytes 1048576 | tf_op jit(solution)/shard_map/all_to_all | solution.py:375
  210.6 40.8 %all-to-all-start.2 = ((bf16[16,256,128]{2,1,0:T(8,128)(2,1)}), bf16[16,256,128]{2,1,0:T(8,128)(2,1)S(1)}, u32[]{:S(2)}, u32[]{:S(2)}) async-start(bf16[16,256,128]{2,1,0:T(8,128)(2,1)} %bitcast.105), calls=%async_computation.2 | async-start | bytes 2097152 | tf_op jit(solution)/shard_map/all_to_all | solution.py:375
  214.4 17.1 %collective-permute-start.17 = (bf16[1,2,128,512]{3,2,1,0:T(8,128)(2,1)S(1)}, bf16[1,2,128,512]{3,2,1,0:T(8,128)(2,1)S(1)}, u32[]{:S(2)}, u32[]{:S(2)}) collective-permute-start(bf16[1,2,128,512]{3,2,1,0:T(8,128)(2,1)S(1)} %constant_dynamic-slice_fusion.3), channel_id=1, source_target_pairs={{0,4},{4,0},{1,5},{5,1},{2,6},{6,2},{3,7},{7,3},{8,12},{12,8},{9,1... | collective-permute-start | bytes 786440 | tf_op jit(solution)/shard_map/ppermute | solution.py:369
  239.7 4.2 %collective-permute-start.19 = (bf16[144,128]{1,0:T(8,128)(2,1)}, bf16[144,128]{1,0:T(8,128)(2,1)S(1)}, u32[]{:S(2)}, u32[]{:S(2)}) collective-permute-start(bf16[144,128]{1,0:T(8,128)(2,1)} %get-tuple-element.27), channel_id=1, source_target_pairs={{0,8},{8,0},{1,9},{9,1},{2,10},{10,2},{3,11},{11,3},{4,12},{12,4},... | collective-permute-start | bytes 110600 | tf_op jit(solution)/shard_map/ppermute | solution.py:358
  243.8 5.6 %collective-permute-start.20 = (bf16[2,144,128]{2,1,0:T(8,128)(2,1)S(1)}, bf16[2,144,128]{2,1,0:T(8,128)(2,1)S(1)}, u32[]{:S(2)}, u32[]{:S(2)}) collective-permute-start(bf16[2,144,128]{2,1,0:T(8,128)(2,1)S(1)} %bitcast_dynamic-update-slice_fusion.9), channel_id=1, source_target_pairs={{0,16},{16,0},{1,17},{17,1},{2,18},{18,2},{3,19},{19,3},{4,20},{20... | collective-permute-start | bytes 221192 | tf_op jit(solution)/shard_map/ppermute | solution.py:358
  249.5 8.1 %collective-permute-start.21 = (bf16[2,2,144,128]{3,2,1,0:T(8,128)(2,1)S(1)}, bf16[2,2,144,128]{3,2,1,0:T(8,128)(2,1)}, u32[]{:S(2)}, u32[]{:S(2)}) collective-permute-start(bf16[2,2,144,128]{3,2,1,0:T(8,128)(2,1)S(1)} %bitcast_dynamic-update-slice_fusion.8), channel_id=1, source_target_pairs={{0,4},{4,0},{1,5},{5,1},{2,6},{6,2},{3,7},{7,3},{8,12},{12,8},{9,1... | collective-permute-start | bytes 442376 | tf_op jit(solution)/shard_map/ppermute | solution.py:358
  251.3 9.1 %copy-start.5 = (bf16[16,256,128]{2,1,0:T(8,128)(2,1)}, bf16[16,256,128]{2,1,0:T(8,128)(2,1)S(1)}, u32[]{:S(2)}) copy-start(bf16[16,256,128]{2,1,0:T(8,128)(2,1)S(1)} %all-to-all-done.2) | copy-start | bytes 3145732
  251.3 19.9 %all-to-all-start.3 = ((bf16[16,128,128]{2,1,0:T(8,128)(2,1)}), bf16[16,128,128]{2,1,0:T(8,128)(2,1)S(1)}, u32[]{:S(2)}, u32[]{:S(2)}) async-start(bf16[16,128,128]{2,1,0:T(8,128)(2,1)} %get-tuple-element.25), calls=%async_computation.3 | async-start | bytes 1048576 | tf_op jit(solution)/shard_map/all_to_all | solution.py:375
  257.0 1.7 collective-permute-start.18
  258.5 2.0 collective-permute-start.22
  (7 other events, 8.2 us)
